TPU v7x, 128 devices: a whole 4x4x4 slice. The times are simulated.
128 devices in a mesh: leaf: 8 (over x, core), front: 16 (over z, y), wave: 1.
Axes of the slice: x: 4, y: 4, z: 4, core: 2. Of those that a mesh axis runs over, the one named last changes fastest.
Arguments:
- sources: float32 [16384, 128], P(('wave', 'front')), may hold values from -48 to 48
- order: int32 [16384], P('front'), may hold values from 0 to 16383, as said below
- diagonal: float32 [16384], P(('wave', 'front')), may hold values from 0.1 to 2
- coupling: float32 [16384, 8192], P(('wave', 'front'), 'leaf'), may hold values from -0.046875 to 0.046875
- interior_inverse: float32 [128, 64, 64], P(('wave', 'leaf')), may hold values from -2 to 6, as said below
- interior_load: float32 [128, 64, 128], P(('wave', 'leaf')), may hold values from -6 to 6
Outputs:
- solution: float32 [16384, 128], P(('wave', 'front'))
- interior_solution: float32 [128, 64, 128], P(('wave', 'leaf'))
Inputs may be any that keep to these rules, and one draw needn't show every extreme that they name: `order`: each aligned block of 1024 entries is a permutation of that block's own indices. `interior_inverse`: each matrix is symmetric positive definite.
All inputs are finite; a program needn't handle non-finite values.
Results may differ from a plain program's by a relative error of at most 0.0003.
Values sent between devices are 32-bit elements; how exact they have to be, the bound alone decides.
A program may use at most 64 MiB of HBM per device.

v0:
```python
import functools

import jax
import jax.numpy as jnp
from jax import lax
from jax.experimental import pallas as pl
from jax.experimental.pallas import tpu as pltpu
from jax.sharding import PartitionSpec as P

ITERS = 4
NZ, NY, NX, CORES = 4, 4, 4, 2
EXTRA = 8
HIGHEST = lax.Precision.HIGHEST
F32 = jnp.float32
BF16 = jnp.bfloat16


def far_first(n):
    return sorted(range(n), key=lambda d: -min(d, n - d))


def split(value):
    high = value.astype(BF16)
    return high, (value - high.astype(F32)).astype(BF16)


def front_solve(
    grid,
    order_ref,
    sources_ref,
    diag_ref,
    coupling_hbm,
    inverse_ref,
    load_ref,
    x_ref,
    interior_ref,
    stage,
    c_high,
    c_low,
    t_high,
    t_low,
    rhs,
    image,
    residual,
    direction,
    diag_full,
    w_send,
    w_recv,
    c_send,
    c_full,
    half_send,
    half_recv,
    share,
    share_recv,
    merged,
    tr_ref,
    td_ref,
    rr_ref,
    q_send,
    q_recv,
    stage_sem,
    w_ssem,
    w_rsem,
    c_ssem,
    c_rsem,
    h_ssem,
    h_rsem,
    s_ssem,
    s_rsem,
    m_ssem,
    m_rsem,
    p_ssem,
    p_rsem,
    q_ssem,
    q_rsem,
):
    nz, ny, nx = grid
    fronts, leaves = nz * ny, nx * CORES
    rows, cols = image.shape
    rank = inverse_ref.shape[1]
    half = rows // 2
    piece = half // nx
    front = lax.axis_index("front")
    leaf = lax.axis_index("leaf")
    z, y = front // ny, front % ny
    x, core = leaf // CORES, leaf % CORES

    z_steps, y_steps, x_steps = far_first(nz), far_first(ny), far_first(nx)
    peers = [(dz, dy) for dz in z_steps for dy in y_steps if dz or dy]

    def front_at(dz, dy):
        return ((z + dz) % nz) * ny + (y + dy) % ny

    def leaf_at(dx):
        return ((x + dx) % nx) * CORES + core

    partner = x * CORES + (1 - core)

    stages = []
    step_rows = rows // stage_sem.shape[0]
    for i in range(stage_sem.shape[0]):
        part = pl.ds(i * step_rows, step_rows)
        stages.append(
            pltpu.make_async_copy(coupling_hbm.at[part], stage.at[part], stage_sem.at[i])
        )
        stages[-1].start()

    barrier = pltpu.get_barrier_semaphore()
    for dz, dy in peers:
        pl.semaphore_signal(barrier, inc=1, device_id={"front": front_at(dz, dy)})
    for d in range(1, leaves):
        pl.semaphore_signal(barrier, inc=1, device_id={"leaf": (leaf + d) % leaves})

    def take(i, _):
        for j in range(8):
            at = i * 8 + j
            image[pl.ds(at, 1), :] = sources_ref[pl.ds(lax.rem(order_ref[at], rows), 1), :]
        return 0

    lax.fori_loop(0, rows // 8, take, 0)

    tile = 128
    for i in range(rows // tile):
        diag_full[i * tile : (i + 1) * tile, :] = jnp.broadcast_to(
            diag_ref[i : i + 1, :], (tile, tile)
        ).T
    zero = jnp.zeros((rows, cols), F32)
    x_ref[...] = zero
    residual[...] = zero
    direction[...] = zero
    tr_ref[...] = jnp.zeros_like(tr_ref)
    td_ref[...] = jnp.zeros_like(td_ref)
    rr_ref[...] = jnp.zeros_like(rr_ref)

    for i, copy in enumerate(stages):
        copy.wait()
        for r in range(i * step_rows, (i + 1) * step_rows, tile):

            def turn(j, _, r=r):
                at = pl.ds(pl.multiple_of(j * tile, tile), tile)
                block = stage[r : r + tile, at]
                high, low = split(block)
                c_high[r : r + tile, at] = high
                c_low[r : r + tile, at] = low
                high, low = split(block.T)
                t_high[at, r : r + tile] = high
                t_low[at, r : r + tile] = low
                return 0

            lax.fori_loop(0, stage.shape[1] // tile, turn, 0)

    def split_rows(i, block):
        high, low = split(block)
        rhs[i : i + tile, 0:cols] = high
        rhs[i : i + tile, cols : 2 * cols] = low

    for i in range(0, rows, tile):
        split_rows(i, image[i : i + tile, :])

    pl.semaphore_wait(barrier, len(peers) + leaves - 1)

    def times(high_ref, low_ref, at):
        both = jnp.dot(high_ref[at, :], rhs[...], preferred_element_type=F32)
        both += jnp.dot(low_ref[at, :], rhs[...], preferred_element_type=F32)
        return both[:, :cols] + both[:, cols:]

    def project(k, is_first, last):
        sums = [jnp.zeros((8, cols), F32)] * 3
        for i in range(0, rows, tile):
            im = image[i : i + tile, :]
            for n, other in enumerate(
                (direction[i : i + tile, :], residual[i : i + tile, :], im)
            ):
                sums[n] = sums[n] + (other * im).reshape(-1, 8, cols).sum(axis=0)
        dots = jnp.concatenate(
            [s.sum(axis=0, keepdims=True) for s in sums] + [jnp.zeros((EXTRA - 3, cols), F32)]
        )
        pending = []
        for dz in z_steps:
            at_z = (z + dz) % nz
            span = ny * rank
            at = pl.ds(pl.multiple_of(at_z * span, span), span)
            out = times(t_high, t_low, at)
            for j in range(ny):
                w_send[at_z * ny + j, 0:rank, :] = out[j * rank : (j + 1) * rank]
                w_send[at_z * ny + j, rank:, :] = dots
            for dy in y_steps:
                if dz or dy:
                    to = front_at(dz, dy)
                    n = dz * ny + dy
                    copy = pltpu.make_async_remote_copy(
                        src_ref=w_send.at[to],
                        dst_ref=w_recv.at[front],
                        send_sem=w_ssem.at[n],
                        recv_sem=w_rsem.at[n],
                        device_id={"front": to},
                    )
                    copy.start()
                    pending.append(copy)
        w_recv[front] = w_send[front]
        for copy in pending:
            copy.wait_recv()
        total = w_recv[0]
        for n in range(1, fronts):
            total = total + w_recv[n]
        w = total[0:rank]
        curvature, cross, square = (total[rank + n : rank + n + 1] for n in range(3))
        rr = rr_ref[...]
        alpha = jnp.where(is_first, -1.0, rr / curvature)
        rr_next = rr - 2.0 * alpha * cross + alpha * alpha * square
        beta = jnp.where(is_first, 0.0, rr_next / rr)
        rr_ref[...] = rr_next
        tr = tr_ref[...] - alpha * w
        td = tr + beta * td_ref[...]
        tr_ref[...] = tr
        td_ref[...] = td
        coeff = jnp.dot(inverse_ref[front], td, precision=HIGHEST, preferred_element_type=F32)

        def advance():
            q = jnp.zeros((8, cols), F32)
            for i in range(0, rows, tile):
                at = slice(i, i + tile)
                x_ref[at, :] += alpha * direction[at, :]
                res = residual[at, :] - alpha * image[at, :]
                residual[at, :] = res
                new = res + beta * direction[at, :]
                direction[at, :] = new
                if last:
                    q = q + (diag_full[at, :] * new * new).reshape(-1, 8, cols).sum(axis=0)
            return q

        c_send[0:rank, :] = coeff
        c_full[k, front, 0:rank, :] = coeff
        if last:
            q = advance() * (1.0 / leaves)
            q = q + (td * coeff).reshape(-1, 8, cols).sum(axis=0)
            c_send[rank:, :] = q
            c_full[k, front, rank:, :] = q
        size = rank + (8 if last else 0)
        spread = []
        for dz, dy in peers:
            n = dz * ny + dy
            copy = pltpu.make_async_remote_copy(
                src_ref=c_send.at[0:size],
                dst_ref=c_full.at[k, front, 0:size],
                send_sem=c_ssem.at[n],
                recv_sem=c_rsem.at[n],
                device_id={"front": front_at(dz, dy)},
            )
            copy.start()
            spread.append(copy)
        if not last:
            advance()
        for copy in pending:
            copy.wait_send()
        return alpha, spread

    def subtract(k, step):
        for n in range(fronts):
            interior_ref[n] = interior_ref[n] - step * c_full[k, n, 0:rank, :]

    def iterate(k, _):
        is_first = k == 0
        alpha, spread = project(k, is_first, False)

        @pl.when(is_first)
        def _():
            for n in range(fronts):
                interior_ref[n] = jnp.dot(
                    inverse_ref[n], load_ref[n], precision=HIGHEST, preferred_element_type=F32
                )

        @pl.when(k > 0)
        def _():
            subtract(k - 1, alpha)

        for copy in spread:
            copy.wait_recv()
        for n in range(fronts):
            high, low = split(c_full[k, n, 0:rank, :])
            rhs[n * rank : (n + 1) * rank, 0:cols] = high
            rhs[n * rank : (n + 1) * rank, cols : 2 * cols] = low

        theirs = pl.multiple_of((1 - core) * half, half)
        mine = pl.multiple_of(core * half, half)
        for i in range(0, half, tile * 2):
            n = min(tile * 2, half)
            half_send[i : i + n, :] = times(c_high, c_low, pl.ds(theirs + i, n))
        over = pltpu.make_async_remote_copy(
            src_ref=half_send,
            dst_ref=half_recv,
            send_sem=h_ssem,
            recv_sem=h_rsem,
            device_id={"leaf": partner},
        )
        over.start()
        for i in range(0, half, tile * 2):
            n = min(tile * 2, half)
            out = times(c_high, c_low, pl.ds(mine + i, n))
            for j in range(0, n, piece):
                share[(i + j) // piece] = out[j : j + piece]
        for copy in spread:
            copy.wait_send()
        over.wait_recv()
        for n in range(nx):
            share[n] = share[n] + half_recv[n * piece : (n + 1) * piece, :]
        moves = []
        for dx in x_steps:
            if dx:
                copy = pltpu.make_async_remote_copy(
                    src_ref=share.at[(x + dx) % nx],
                    dst_ref=share_recv.at[x],
                    send_sem=s_ssem.at[dx],
                    recv_sem=s_rsem.at[dx],
                    device_id={"leaf": leaf_at(dx)},
                )
                copy.start()
                moves.append(copy)
        share_recv[x] = share[x]
        for copy in moves:
            copy.wait_recv()
        total = share_recv[0]
        for n in range(1, nx):
            total = total + share_recv[n]
        own = core * nx + x
        merged[own] = total
        out_x = []
        for dx in x_steps:
            if dx:
                copy = pltpu.make_async_remote_copy(
                    src_ref=merged.at[own],
                    dst_ref=merged.at[own],
                    send_sem=m_ssem.at[dx],
                    recv_sem=m_rsem.at[dx],
                    device_id={"leaf": leaf_at(dx)},
                )
                copy.start()
                out_x.append((dx, copy))

        def pass_on(dx):
            at = core * nx + (x - dx + nx) % nx
            copy = pltpu.make_async_remote_copy(
                src_ref=merged.at[at],
                dst_ref=merged.at[at],
                send_sem=p_ssem.at[dx],
                recv_sem=p_rsem.at[dx],
                device_id={"leaf": partner},
            )
            copy.start()
            return copy

        passed = [pass_on(0)]
        for copy in moves:
            copy.wait_send()
        over.wait_send()
        for dx, copy in reversed(out_x):
            copy.wait_recv()
            passed.append(pass_on(dx))
        for copy in passed:
            copy.wait_recv()
        for n in range(rows // piece):
            at = slice(n * piece, (n + 1) * piece)
            new = diag_full[at, :] * direction[at, :] + merged[n]
            image[at, :] = new
            high, low = split(new)
            rhs[at, 0:cols] = high
            rhs[at, cols : 2 * cols] = low
        for dx, copy in out_x:
            copy.wait_send()
        for copy in passed:
            copy.wait_send()
        return 0

    lax.fori_loop(0, ITERS - 1, iterate, 0)

    end = ITERS - 1
    alpha, spread = project(end, False, True)
    subtract(end - 1, alpha)
    for copy in spread:
        copy.wait_recv()
    q = c_full[end, 0, rank:, :]
    for n in range(1, fronts):
        q = q + c_full[end, n, rank:, :]
    q_send[...] = q
    q_recv[leaf] = q
    last_sums = []
    for d in range(1, leaves):
        copy = pltpu.make_async_remote_copy(
            src_ref=q_send,
            dst_ref=q_recv.at[leaf],
            send_sem=q_ssem.at[d],
            recv_sem=q_rsem.at[d],
            device_id={"leaf": (leaf + d) % leaves},
        )
        copy.start()
        last_sums.append(copy)
    for copy in spread:
        copy.wait_send()
    for copy in last_sums:
        copy.wait_recv()
    q = q_recv[0]
    for n in range(1, leaves):
        q = q + q_recv[n]
    step = rr_ref[...] / q.sum(axis=0, keepdims=True)
    for i in range(0, rows, tile):
        at = slice(i, i + tile)
        x_ref[at, :] += step * direction[at, :]
    subtract(end, step)
    for copy in last_sums:
        copy.wait_send()


def per_device(sources, order, diagonal, coupling, interior_inverse, interior_load, grid=(NZ, NY, NX)):
    nz, ny, nx = grid
    fronts, leaves = nz * ny, nx * CORES
    rows, cols = sources.shape
    depth = coupling.shape[1]
    blocks, rank = interior_inverse.shape[:2]
    assert blocks == fronts and depth == blocks * rank
    piece = rows // 2 // nx
    vmem = pl.BlockSpec(memory_space=pltpu.VMEM)
    dma = pltpu.SemaphoreType.DMA
    field = pltpu.VMEM((rows, cols), F32)
    return tuple(
        pl.pallas_call(
            functools.partial(front_solve, grid),
            out_shape=(
                jax.ShapeDtypeStruct((rows, cols), F32),
                jax.ShapeDtypeStruct(interior_load.shape, F32),
            ),
            in_specs=[
                pl.BlockSpec(memory_space=pltpu.SMEM),
                vmem,
                vmem,
                pl.BlockSpec(memory_space=pl.ANY),
                vmem,
                vmem,
            ],
            out_specs=(vmem, vmem),
            scratch_shapes=[
                pltpu.VMEM((rows, depth), F32),
                pltpu.VMEM((rows, depth), BF16),
                pltpu.VMEM((rows, depth), BF16),
                pltpu.VMEM((depth, rows), BF16),
                pltpu.VMEM((depth, rows), BF16),
                pltpu.VMEM((max(rows, depth), 2 * cols), BF16),
                field,
                field,
                field,
                field,
                pltpu.VMEM((fronts, rank + EXTRA, cols), F32),
                pltpu.VMEM((fronts, rank + EXTRA, cols), F32),
                pltpu.VMEM((rank + EXTRA, cols), F32),
                pltpu.VMEM((ITERS, fronts, rank + EXTRA, cols), F32),
                pltpu.VMEM((rows // 2, cols), F32),
                pltpu.VMEM((rows // 2, cols), F32),
                pltpu.VMEM((nx, piece, cols), F32),
                pltpu.VMEM((nx, piece, cols), F32),
                pltpu.VMEM((CORES * nx, piece, cols), F32),
                pltpu.VMEM((rank, cols), F32),
                pltpu.VMEM((rank, cols), F32),
                pltpu.VMEM((1, cols), F32),
                pltpu.VMEM((8, cols), F32),
                pltpu.VMEM((leaves, 8, cols), F32),
                dma((min(4, rows // 128),)),
                dma((fronts,)),
                dma((fronts,)),
                dma((fronts,)),
                dma((fronts,)),
                dma,
                dma,
                dma((nx,)),
                dma((nx,)),
                dma((nx,)),
                dma((nx,)),
                dma((nx,)),
                dma((nx,)),
                dma((leaves,)),
                dma((leaves,)),
            ],
            compiler_params=pltpu.CompilerParams(
                collective_id=0, has_side_effects=True, vmem_limit_bytes=48 << 20
            ),
            name="front_solve",
        )(
            order,
            sources,
            diagonal.reshape(rows // 128, 128),
            coupling,
            interior_inverse,
            interior_load,
        )
    )


def solution(mesh):
    in_specs = (
        P(("wave", "front"), None),
        P("front"),
        P(("wave", "front")),
        P(("wave", "front"), "leaf"),
        P(("wave", "leaf"), None, None),
        P(("wave", "leaf"), None, None),
    )
    out_specs = (P(("wave", "front"), None), P(("wave", "leaf"), None, None))
    return jax.shard_map(
        per_device, mesh=mesh, in_specs=in_specs, out_specs=out_specs, check_vma=False
    )
```

profile of v0, /device:TPU:1, one launch (start us, length us, event | category | flops | bytes accessed | tf_op | source)
XLA Modules:
  0.0 143.2 jit_solution(2221302744674713927)
XLA Ops:
  0.6 0.0 copy-start
  0.6 1.0 copy-done
  1.7 0.0 copy-start.1
  1.7 1.0 copy-done.1
  2.7 0.0 copy-start.2
  2.7 1.0 copy-done.2
  3.8 0.0 copy-start.3
  3.8 0.7 copy-done.3
  4.4 0.0 copy-start.4
  4.4 0.7 copy-done.4
  5.1 136.5 %front_solve.1 = (f32[1024,128]{1,0:T(8,128)S(1)}, f32[16,64,128]{2,1,0:T(8,128)S(1)}) custom-call(s32[1024]{0:T(1024)S(1)} %copy-done.3, f32[1024,128]{1,0:T(8,128)S(1)} %copy-done, f32[8,128]{1,0:T(8,128)S(1)} %bitcast.1, f32[1024,1024]{1,0:T(8,128)} %coupling_hbm.1, f32[16,64,64]{2,1,0:T(8,128)S(1)} %copy-done.1, f32[16,64,128]{2,1,0:T(8,128)S(1)} %copy-done.2), custom_call_target="tpu_custom_call" | custom-call | tf_op jit(solution)/shard_map/front_solve/pallas_call | solution.py:425
  141.7 0.8 copy.10
  142.5 0.8 copy.11
Async XLA Ops:
  0.6 1.0 copy-start
  1.7 1.0 copy-start.1
  2.7 1.0 copy-start.2
  3.8 0.7 copy-start.3
  4.4 0.7 copy-start.4
where the time goes:
time: 144 us; the launch traced here: 143 us
  Pallas kernels  137 us (95%)
  local copies, waits for them, and re-layouts  6.08 us (4%)
    pallas_call x1, Pallas kernels, per_device(): pl.pallas_call(functools.partial(front_solve, grid), out_shape=(jax.Shape...  137 us
    unnamed x12, local copies, waits for them, and re-layouts  6.08 us

commit v1 on v0

v1 whole, which is shorter than its diff:
```python
import functools

import jax
import jax.numpy as jnp
from jax import lax
from jax.experimental import pallas as pl
from jax.experimental.pallas import tpu as pltpu
from jax.sharding import PartitionSpec as P

ITERS = 4
NZ, NY, NX, CORES = 4, 4, 4, 2
EXTRA = 8
SUMS = 3
HIGHEST = lax.Precision.HIGHEST
F32 = jnp.float32
BF16 = jnp.bfloat16


def far_first(n):
    return sorted(range(n), key=lambda d: -min(d, n - d))


def split(value):
    high = value.astype(BF16)
    return high, (value - high.astype(F32)).astype(BF16)


def front_solve(
    grid,
    order_hbm,
    sources_hbm,
    diag_hbm,
    coupling_hbm,
    inverse_hbm,
    load_hbm,
    x_ref,
    direction,
    interior_ref,
    last_ref,
    step_ref,
    order_ref,
    sources_ref,
    diag_ref,
    inverse_ref,
    load_ref,
    stage,
    c_high,
    c_low,
    t_high,
    t_low,
    rhs,
    turned,
    image,
    residual,
    diag_full,
    w_send,
    w_recv,
    c_send,
    c_full,
    half_send,
    half_recv,
    share,
    share_recv,
    merged,
    tr_ref,
    td_ref,
    rr_ref,
    q_send,
    q_recv,
    g_send,
    g_recv,
    load_sem,
    stage_sem,
    w_ssem,
    w_rsem,
    c_ssem,
    c_rsem,
    h_ssem,
    h_rsem,
    s_ssem,
    s_rsem,
    m_ssem,
    m_rsem,
    p_ssem,
    p_rsem,
    q_ssem,
    q_rsem,
    g_ssem,
    g_rsem,
):
    nz, ny, nx = grid
    fronts, leaves = nz * ny, nx * CORES
    rows, cols = image.shape
    rank = inverse_ref.shape[1]
    half = rows // 2
    piece = half // nx
    front = lax.axis_index("front")
    leaf = lax.axis_index("leaf")
    z, y = front // ny, front % ny
    x, core = leaf // CORES, leaf % CORES

    z_steps, y_steps, x_steps = far_first(nz), far_first(ny), far_first(nx)
    peers = [(dz, dy) for dz in z_steps for dy in y_steps if dz or dy]

    def front_at(dz, dy):
        return ((z + dz) % nz) * ny + (y + dy) % ny

    def leaf_at(dx):
        return ((x + dx) % nx) * CORES + core

    partner = x * CORES + (1 - core)

    loads = [
        pltpu.make_async_copy(source, here, load_sem.at[i])
        for i, (source, here) in enumerate(
            (
                (order_hbm, order_ref),
                (sources_hbm, sources_ref),
                (diag_hbm, diag_ref),
                (inverse_hbm, inverse_ref),
                (load_hbm, load_ref),
            )
        )
    ]
    for copy in loads[:2]:
        copy.start()
    stages = []
    step_rows = rows // stage_sem.shape[0]
    for i in range(stage_sem.shape[0]):
        part = pl.ds(i * step_rows, step_rows)
        stages.append(
            pltpu.make_async_copy(coupling_hbm.at[part], stage.at[part], stage_sem.at[i])
        )
        stages[-1].start()
    for copy in loads[2:]:
        copy.start()

    barrier = pltpu.get_barrier_semaphore()
    for dz, dy in peers:
        pl.semaphore_signal(barrier, inc=1, device_id={"front": front_at(dz, dy)})
    for d in range(1, leaves):
        pl.semaphore_signal(barrier, inc=1, device_id={"leaf": (leaf + d) % leaves})

    tile = 128
    for copy in loads[:2]:
        copy.wait()

    def take(i, _):
        for j in range(16):
            at = i * 16 + j
            image[pl.ds(at, 1), :] = sources_ref[pl.ds(order_ref[at] & (rows - 1), 1), :]
        return 0

    lax.fori_loop(0, rows // 16, take, 0)
    for i in range(0, rows, tile):
        high, low = split(image[i : i + tile, :].T)
        turned[0:cols, i : i + tile] = high
        turned[cols:, i : i + tile] = low
    x_ref[...] = jnp.zeros((rows, cols), F32)

    for i, copy in enumerate(stages):
        copy.wait()

        def divide(j, _, i=i):
            at = pl.ds(pl.multiple_of(i * step_rows + j * 16, 16), 16)
            high, low = split(stage[at, :])
            c_high[at, :] = high
            c_low[at, :] = low
            return 0

        lax.fori_loop(0, step_rows // 16, divide, 0)

    def turn(start, stop):
        def columns(j, _):
            for r in range(start, stop, tile):
                at = pl.ds(pl.multiple_of(j * tile, tile), tile)
                high, low = split(stage[r : r + tile, at].T)
                t_high[at, r : r + tile] = high
                t_low[at, r : r + tile] = low
            return 0

        lax.fori_loop(0, stage.shape[1] // tile, columns, 0)

    def spread_diagonal():
        for i in range(rows // tile):
            diag_full[i * tile : (i + 1) * tile, :] = jnp.broadcast_to(
                diag_ref[i : i + 1, :], (tile, tile)
            ).T

    def start_interior():
        for n in range(fronts):
            interior_ref[n * rank : (n + 1) * rank, :] = jnp.dot(
                inverse_ref[n], load_ref[n], precision=HIGHEST, preferred_element_type=F32
            )

    pl.semaphore_wait(barrier, len(peers) + leaves - 1)

    def times(high_ref, low_ref, at):
        both = jnp.dot(high_ref[at, :], rhs[...], preferred_element_type=F32)
        both += jnp.dot(low_ref[at, :], rhs[...], preferred_element_type=F32)
        return both[:, :cols] + both[:, cols:]

    def times_turned(at):
        both = jnp.dot(turned[...], c_high[:, at], preferred_element_type=F32)
        both += jnp.dot(turned[...], c_low[:, at], preferred_element_type=F32)
        both = both[:cols] + both[cols:]
        n = both.shape[1]
        return jnp.concatenate([both[:, i : i + tile].T for i in range(0, n, tile)])

    def project(k, is_first, last):
        sums = [jnp.zeros((8, cols), F32)] * SUMS
        for i in range(0, rows, tile):
            im = image[i : i + tile, :]
            others = (im, im, im) if is_first else (direction[i : i + tile, :], residual[i : i + tile, :], im)
            for n, other in enumerate(others):
                sums[n] = sums[n] + (other * im).reshape(-1, 8, cols).sum(axis=0)
        dots = jnp.concatenate(
            [s.sum(axis=0, keepdims=True) for s in sums] + [jnp.zeros((EXTRA - SUMS, cols), F32)]
        )
        pending = []
        for dz in z_steps:
            at_z = (z + dz) % nz
            span = ny * rank
            at = pl.ds(pl.multiple_of(at_z * span, span), span)
            out = times_turned(at) if is_first else times(t_high, t_low, at)
            for j in range(ny):
                w_send[at_z * ny + j, 0:rank, :] = out[j * rank : (j + 1) * rank]
                w_send[at_z * ny + j, rank:, :] = dots
            for dy in y_steps:
                if dz or dy:
                    to = front_at(dz, dy)
                    n = dz * ny + dy
                    copy = pltpu.make_async_remote_copy(
                        src_ref=w_send.at[to, 0 : rank + SUMS],
                        dst_ref=w_recv.at[front, 0 : rank + SUMS],
                        send_sem=w_ssem.at[n],
                        recv_sem=w_rsem.at[n],
                        device_id={"front": to},
                    )
                    copy.start()
                    pending.append(copy)
        w_recv[front, 0 : rank + SUMS, :] = w_send[front, 0 : rank + SUMS, :]
        if is_first:
            turn(0, rows // 2)
            loads[3].wait()
        for copy in pending:
            copy.wait_recv()
        w = w_recv[0, 0:rank, :]
        curvature, cross, square = (w_recv[0, rank + n : rank + n + 1, :] for n in range(SUMS))
        for n in range(1, fronts):
            w = w + w_recv[n, 0:rank, :]
            curvature = curvature + w_recv[n, rank : rank + 1, :]
            cross = cross + w_recv[n, rank + 1 : rank + 2, :]
            square = square + w_recv[n, rank + 2 : rank + 3, :]
        if is_first:
            alpha = beta = None
            rr_ref[...] = square
            tr = td = w
        else:
            rr = rr_ref[...]
            alpha = rr / curvature
            rr_next = rr - 2.0 * alpha * cross + alpha * alpha * square
            beta = rr_next / rr
            rr_ref[...] = rr_next
            tr = tr_ref[...] - alpha * w
            td = tr + beta * td_ref[...]
        tr_ref[...] = tr
        td_ref[...] = td
        coeff = jnp.dot(inverse_ref[front], td, precision=HIGHEST, preferred_element_type=F32)

        here = c_full.at[k] if not last else last_ref
        rows_here = pl.ds(pl.multiple_of(front * rank, rank), rank)
        c_send[...] = coeff
        here[rows_here, :] = coeff
        spread = []
        for dz, dy in peers:
            n = dz * ny + dy
            copy = pltpu.make_async_remote_copy(
                src_ref=c_send,
                dst_ref=here.at[rows_here],
                send_sem=c_ssem.at[n],
                recv_sem=c_rsem.at[n],
                device_id={"front": front_at(dz, dy)},
            )
            copy.start()
            spread.append(copy)
        own = (td * coeff).reshape(-1, 8, cols).sum(axis=0) if last else None
        return alpha, beta, own, spread, pending

    def advance(alpha, beta):
        for i in range(0, rows, tile):
            at = slice(i, i + tile)
            x_ref[at, :] += alpha * direction[at, :]
            res = residual[at, :] - alpha * image[at, :]
            residual[at, :] = res
            direction[at, :] = res + beta * direction[at, :]

    def subtract(k, step):
        for i in range(0, fronts * rank, tile):
            at = slice(i, i + tile)
            interior_ref[at, :] = interior_ref[at, :] - step * c_full[k, at, :]

    def iterate(k, is_first):
        alpha, beta, _, spread, pending = project(k, is_first, False)
        if is_first:
            residual[...] = image[...]
            direction[...] = image[...]
            for copy in (loads[2], loads[4]):
                copy.wait()
            turn(rows // 2, rows)
            spread_diagonal()
            start_interior()
        else:
            advance(alpha, beta)
            subtract(k - 1, alpha)
        for copy in pending:
            copy.wait_send()

        for copy in spread:
            copy.wait_recv()
        for i in range(0, fronts * rank, tile):
            high, low = split(c_full[k, i : i + tile, :])
            rhs[i : i + tile, 0:cols] = high
            rhs[i : i + tile, cols : 2 * cols] = low

        theirs = pl.multiple_of((1 - core) * half, half)
        mine = pl.multiple_of(core * half, half)
        for i in range(0, half, tile * 2):
            n = min(tile * 2, half)
            half_send[i : i + n, :] = times(c_high, c_low, pl.ds(theirs + i, n))
        over = pltpu.make_async_remote_copy(
            src_ref=half_send,
            dst_ref=half_recv,
            send_sem=h_ssem,
            recv_sem=h_rsem,
            device_id={"leaf": partner},
        )
        over.start()
        for i in range(0, half, tile * 2):
            n = min(tile * 2, half)
            out = times(c_high, c_low, pl.ds(mine + i, n))
            for j in range(0, n, piece):
                share[(i + j) // piece] = out[j : j + piece]
        for copy in spread:
            copy.wait_send()
        over.wait_recv()
        for n in range(nx):
            share[n] = share[n] + half_recv[n * piece : (n + 1) * piece, :]
        moves = []
        for dx in x_steps:
            if dx:
                copy = pltpu.make_async_remote_copy(
                    src_ref=share.at[(x + dx) % nx],
                    dst_ref=share_recv.at[x],
                    send_sem=s_ssem.at[dx],
                    recv_sem=s_rsem.at[dx],
                    device_id={"leaf": leaf_at(dx)},
                )
                copy.start()
                moves.append(copy)
        share_recv[x] = share[x]
        for copy in moves:
            copy.wait_recv()
        total = share_recv[0]
        for n in range(1, nx):
            total = total + share_recv[n]
        own = core * nx + x
        merged[own] = total
        out_x = []
        for dx in x_steps:
            if dx:
                copy = pltpu.make_async_remote_copy(
                    src_ref=merged.at[own],
                    dst_ref=merged.at[own],
                    send_sem=m_ssem.at[dx],
                    recv_sem=m_rsem.at[dx],
                    device_id={"leaf": leaf_at(dx)},
                )
                copy.start()
                out_x.append((dx, copy))

        def pass_on(dx):
            at = core * nx + (x - dx + nx) % nx
            copy = pltpu.make_async_remote_copy(
                src_ref=merged.at[at],
                dst_ref=merged.at[at],
                send_sem=p_ssem.at[dx],
                recv_sem=p_rsem.at[dx],
                device_id={"leaf": partner},
            )
            copy.start()
            return copy

        passed = [pass_on(0)]
        for copy in moves:
            copy.wait_send()
        over.wait_send()
        for dx, copy in reversed(out_x):
            copy.wait_recv()
            passed.append(pass_on(dx))
        for copy in passed:
            copy.wait_recv()
        for n in range(rows // piece):
            at = slice(n * piece, (n + 1) * piece)
            new = diag_full[at, :] * direction[at, :] + merged[n]
            image[at, :] = new
            high, low = split(new)
            rhs[at, 0:cols] = high
            rhs[at, cols : 2 * cols] = low
        for dx, copy in out_x:
            copy.wait_send()
        for copy in passed:
            copy.wait_send()
        return 0

    iterate(0, True)
    lax.fori_loop(1, ITERS - 1, lambda k, _: iterate(k, False), 0)

    end = ITERS - 1
    alpha, beta, own, spread, pending = project(end, False, True)
    q_send[...] = own
    q_recv[leaf] = own
    over_leaf = []
    for d in range(1, leaves):
        copy = pltpu.make_async_remote_copy(
            src_ref=q_send,
            dst_ref=q_recv.at[leaf],
            send_sem=q_ssem.at[d],
            recv_sem=q_rsem.at[d],
            device_id={"leaf": (leaf + d) % leaves},
        )
        copy.start()
        over_leaf.append(copy)
    advance(alpha, beta)
    q = jnp.zeros((8, cols), F32)
    for i in range(0, rows, tile):
        new = direction[i : i + tile, :]
        q = q + (diag_full[i : i + tile, :] * new * new).reshape(-1, 8, cols).sum(axis=0)
    for copy in over_leaf:
        copy.wait_recv()
    for n in range(leaves):
        q = q + q_recv[n]
    g_send[...] = q
    g_recv[front] = q
    over_front = []
    for dz, dy in peers:
        n = dz * ny + dy
        copy = pltpu.make_async_remote_copy(
            src_ref=g_send,
            dst_ref=g_recv.at[front],
            send_sem=g_ssem.at[n],
            recv_sem=g_rsem.at[n],
            device_id={"front": front_at(dz, dy)},
        )
        copy.start()
        over_front.append(copy)
    subtract(end - 1, alpha)
    for copy in pending + over_leaf:
        copy.wait_send()
    for copy in spread + over_front:
        copy.wait_recv()
    q = g_recv[0]
    for n in range(1, fronts):
        q = q + g_recv[n]
    step_ref[...] = rr_ref[...] / q.sum(axis=0, keepdims=True)
    for copy in spread + over_front:
        copy.wait_send()


def per_device(sources, order, diagonal, coupling, interior_inverse, interior_load, grid=(NZ, NY, NX)):
    nz, ny, nx = grid
    fronts, leaves = nz * ny, nx * CORES
    rows, cols = sources.shape
    depth = coupling.shape[1]
    blocks, rank = interior_inverse.shape[:2]
    assert blocks == fronts and depth == blocks * rank
    piece = rows // 2 // nx
    vmem = pl.BlockSpec(memory_space=pltpu.VMEM)
    dma = pltpu.SemaphoreType.DMA
    field = pltpu.VMEM((rows, cols), F32)
    hbm = pl.BlockSpec(memory_space=pltpu.HBM)
    whole = jax.ShapeDtypeStruct((rows, cols), F32)
    inner = jax.ShapeDtypeStruct((depth, cols), F32)
    x, direction, interior, coeff, step = pl.pallas_call(
        functools.partial(front_solve, grid),
        out_shape=(whole, whole, inner, inner, jax.ShapeDtypeStruct((1, cols), F32)),
        in_specs=[hbm] * 6,
        out_specs=(vmem,) * 5,
        scratch_shapes=[
            pltpu.SMEM((rows,), jnp.int32),
            field,
            pltpu.VMEM((rows // 128, 128), F32),
            pltpu.VMEM(interior_inverse.shape, F32),
            pltpu.VMEM(interior_load.shape, F32),
            pltpu.VMEM((rows, depth), F32),
            pltpu.VMEM((rows, depth), BF16),
            pltpu.VMEM((rows, depth), BF16),
            pltpu.VMEM((depth, rows), BF16),
            pltpu.VMEM((depth, rows), BF16),
            pltpu.VMEM((max(rows, depth), 2 * cols), BF16),
            pltpu.VMEM((2 * cols, rows), BF16),
            field,
            field,
            field,
            pltpu.VMEM((fronts, rank + EXTRA, cols), F32),
            pltpu.VMEM((fronts, rank + EXTRA, cols), F32),
            pltpu.VMEM((rank, cols), F32),
            pltpu.VMEM((ITERS - 1, depth, cols), F32),
            pltpu.VMEM((rows // 2, cols), F32),
            pltpu.VMEM((rows // 2, cols), F32),
            pltpu.VMEM((nx, piece, cols), F32),
            pltpu.VMEM((nx, piece, cols), F32),
            pltpu.VMEM((CORES * nx, piece, cols), F32),
            pltpu.VMEM((rank, cols), F32),
            pltpu.VMEM((rank, cols), F32),
            pltpu.VMEM((1, cols), F32),
            pltpu.VMEM((8, cols), F32),
            pltpu.VMEM((leaves, 8, cols), F32),
            pltpu.VMEM((8, cols), F32),
            pltpu.VMEM((fronts, 8, cols), F32),
            dma((5,)),
            dma((min(8, rows // 128),)),
            dma((fronts,)),
            dma((fronts,)),
            dma((fronts,)),
            dma((fronts,)),
            dma,
            dma,
            dma((nx,)),
            dma((nx,)),
            dma((nx,)),
            dma((nx,)),
            dma((nx,)),
            dma((nx,)),
            dma((leaves,)),
            dma((leaves,)),
            dma((fronts,)),
            dma((fronts,)),
        ],
        compiler_params=pltpu.CompilerParams(
            collective_id=0, has_side_effects=True, vmem_limit_bytes=48 << 20
        ),
        name="front_solve",
    )(
        *(
            pltpu.with_memory_space_constraint(value, pltpu.HBM)
            for value in (
                order,
                sources,
                diagonal.reshape(rows // 128, 128),
                coupling,
                interior_inverse,
                interior_load,
            )
        )
    )
    interior = interior - step * coeff
    return x + step * direction, interior.reshape(interior_load.shape)


def solution(mesh):
    in_specs = (
        P(("wave", "front"), None),
        P("front"),
        P(("wave", "front")),
        P(("wave", "front"), "leaf"),
        P(("wave", "leaf"), None, None),
        P(("wave", "leaf"), None, None),
    )
    out_specs = (P(("wave", "front"), None), P(("wave", "leaf"), None, None))
    return jax.shard_map(
        per_device, mesh=mesh, in_specs=in_specs, out_specs=out_specs, check_vma=False
    )
```

time: 144 us -> 127 us (0.88)
  Pallas kernels: 137 us -> 125 us
  local copies, waits for them, and re-layouts: 6.08 us -> 0 us
    pallas_call x1, Pallas kernels: 137 us -> 125 us  [per_device(): pl.pallas_call(functools.partial(front_solve, grid), out_shape=(whole, wh...]
    unnamed x12 -> x0, local copies, waits for them, and re-layouts: 6.08 us -> none
where the time goes in v1:
time: 127 us; the launch traced here: 126 us
  Pallas kernels  125 us (98%)
    pallas_call x1, Pallas kernels, per_device(): pl.pallas_call(functools.partial(front_solve, grid), out_shape=(whole, wh...  125 us

profile of v1, /device:TPU:1, one launch (start us, length us, event | category | flops | bytes accessed | tf_op | source)
XLA Modules:
  0.0 126.5 jit_solution(6085658500664984400)
XLA Ops:
  0.6 124.7 %front_solve.1 = (f32[1024,128]{1,0:T(8,128)S(1)}, f32[1024,128]{1,0:T(8,128)S(1)}, f32[1024,128]{1,0:T(8,128)S(1)}, f32[1024,128]{1,0:T(8,128)S(1)}, f32[1,128]{1,0:T(1,128)S(1)}) custom-call(s32[1024]{0:T(1024)} %order_hbm.1, f32[1024,128]{1,0:T(8,128)} %sources_hbm.1, f32[8,128]{1,0:T(8,128)} %bitcast.5, f32[1024,1024]{1,0:T(8,128)} %coupling_hbm.1, ...), custom_call_target="tpu_custom_call" | custom-call | tf_op jit(solution)/shard_map/front_solve/pallas_call | solution.py:484
  125.4 1.1 multiply_subtract_fusion

commit v2 on v1

v2 whole, which is shorter than its diff:
```python
import functools

import jax
import jax.numpy as jnp
from jax import lax
from jax.experimental import pallas as pl
from jax.experimental.pallas import tpu as pltpu
from jax.sharding import PartitionSpec as P

ITERS = 4
NZ, NY, NX, CORES = 4, 4, 4, 2
EXTRA = 8
SUMS = 3
STREAMS = 2
HIGHEST = lax.Precision.HIGHEST
F32 = jnp.float32
BF16 = jnp.bfloat16


def far_first(n):
    return sorted(range(n), key=lambda d: -min(d, n - d))


def split(value):
    high = value.astype(BF16)
    return high, (value - high.astype(F32)).astype(BF16)


def front_solve(
    grid,
    order_hbm,
    sources_hbm,
    diag_hbm,
    coupling_hbm,
    inverse_hbm,
    load_hbm,
    x_out,
    direction_out,
    interior_out,
    last_out,
    step_ref,
    order_ref,
    sources_ref,
    diag_ref,
    inverse_ref,
    load_ref,
    stage,
    c_high,
    c_low,
    t_high,
    t_low,
    rhs,
    turned,
    loads_ref,
    x_ref,
    image,
    residual,
    direction,
    interior,
    diag_full,
    w_send,
    w_recv,
    c_send,
    c_full,
    half_send,
    half_recv,
    far_send,
    far_recv,
    own_part,
    near_send,
    near_recv,
    merged,
    piece_sums,
    tr_ref,
    td_ref,
    rr_ref,
    q_send,
    q_recv,
    g_send,
    g_recv,
    load_sem,
    stage_sem,
    w_ssem,
    w_rsem,
    c_ssem,
    c_rsem,
    h_ssem,
    h_rsem,
    f_ssem,
    f_rsem,
    n_ssem,
    n_rsem,
    m_ssem,
    m_rsem,
    p_ssem,
    p_rsem,
    q_ssem,
    q_rsem,
    g_ssem,
    g_rsem,
):
    nz, ny, nx = grid
    fronts, leaves = nz * ny, nx * CORES
    rows, cols = loads_ref.shape
    depth = stage.shape[1]
    rank = inverse_ref.shape[1]
    piece = rows // 2 // nx
    tile, lanes = 128, cols // 2
    half_rank, half_piece = rank // 2, piece // 2
    streams = range(STREAMS)
    front = lax.axis_index("front")
    leaf = lax.axis_index("leaf")
    z, y = front // ny, front % ny
    x, core = leaf // CORES, leaf % CORES
    partner, other = x * CORES + (1 - core), 1 - core

    z_steps, y_steps = far_first(nz), far_first(ny)
    far = nx // 2
    near = [d for d in range(1, nx) if d != far]
    peers = [(dz, dy) for dz in z_steps for dy in y_steps if dz or dy]

    def front_at(dz, dy):
        return ((z + dz) % nz) * ny + (y + dy) % ny

    def leaf_at(dx, at_core):
        return ((x + dx) % nx) * CORES + at_core

    def piece_at(dx, at_core):
        return at_core * nx + (x + dx) % nx

    def remote(source, target, sems, at, **place):
        return pltpu.make_async_remote_copy(
            src_ref=source,
            dst_ref=target,
            send_sem=sems[0].at[at],
            recv_sem=sems[1].at[at],
            device_id=place,
        )

    def send(*args, **place):
        copy = remote(*args, **place)
        copy.start()
        return copy

    def swap(value):
        return pltpu.roll(value, lanes, 1)

    def select(a, b):
        return jnp.where(lax.broadcasted_iota(jnp.int32, a.shape, 1) < lanes, a, b)

    def packed(value, s):
        top, bottom = jnp.split(value, 2)
        return select(top, swap(bottom)) if s == 0 else select(swap(top), bottom)

    def full(a, b):
        return jnp.concatenate([select(a, swap(b)), select(swap(a), b)])

    def fold(products):
        top, bottom = jnp.split(products + swap(products), 2)
        return select(top, bottom)

    def operand(value):
        high = value.astype(BF16).astype(F32)
        low = value - high
        return jnp.concatenate([select(high, swap(low)), select(swap(high), low)]).astype(BF16)

    def both_sides(row):
        return row + swap(row)

    loads = [
        pltpu.make_async_copy(source, here, load_sem.at[i])
        for i, (source, here) in enumerate(
            (
                (order_hbm, order_ref),
                (sources_hbm, sources_ref),
                (diag_hbm, diag_ref),
                (inverse_hbm, inverse_ref),
                (load_hbm, load_ref),
            )
        )
    ]
    for copy in loads[:2]:
        copy.start()
    stages = []
    step_rows = rows // stage_sem.shape[0]
    for i in range(stage_sem.shape[0]):
        part = pl.ds(i * step_rows, step_rows)
        stages.append(
            pltpu.make_async_copy(coupling_hbm.at[part], stage.at[part], stage_sem.at[i])
        )
        stages[-1].start()
    for copy in loads[2:]:
        copy.start()

    barrier = pltpu.get_barrier_semaphore()
    for dz, dy in peers:
        pl.semaphore_signal(barrier, inc=1, device_id={"front": front_at(dz, dy)})
    for d in range(1, leaves):
        pl.semaphore_signal(barrier, inc=1, device_id={"leaf": (leaf + d) % leaves})

    def products(s, n, im, others):
        for i, field in enumerate(others):
            piece_sums[s, n, i] = (field * im).reshape(-1, 8, cols).sum(axis=0)

    for copy in loads[:2]:
        copy.wait()

    def take(i, _):
        for j in range(16):
            at = i * 16 + j
            loads_ref[pl.ds(at, 1), :] = sources_ref[pl.ds(order_ref[at] & (rows - 1), 1), :]
        return 0

    lax.fori_loop(0, rows // 16, take, 0)
    for i in range(0, rows, tile):
        high, low = split(loads_ref[i : i + tile, :].T)
        turned[0:cols, i : i + tile] = high
        turned[cols:, i : i + tile] = low

    def start_fields(n, _):
        block = loads_ref[pl.ds(pl.multiple_of(n * piece, piece), piece), :]
        at = pl.ds(pl.multiple_of(n * half_piece, half_piece), half_piece)
        for s in streams:
            value = packed(block, s)
            image[s, at, :] = value
            residual[s, at, :] = value
            direction[s, at, :] = value
            x_ref[s, at, :] = jnp.zeros_like(value)
            products(s, n, value, (value,) * SUMS)
        return 0

    lax.fori_loop(0, rows // piece, start_fields, 0)

    for i, copy in enumerate(stages):
        copy.wait()

        def divide(j, _, i=i):
            at = pl.ds(pl.multiple_of(i * step_rows + j * 16, 16), 16)
            high, low = split(stage[at, :])
            c_high[at, :] = high
            c_low[at, :] = low
            return 0

        lax.fori_loop(0, step_rows // 16, divide, 0)

    def turn(start, stop):
        def columns(j, _):
            for r in range(start, stop, tile):
                at = pl.ds(pl.multiple_of(j * tile, tile), tile)
                high, low = split(stage[r : r + tile, at].T)
                t_high[at, r : r + tile] = high
                t_low[at, r : r + tile] = low
            return 0

        lax.fori_loop(0, depth // tile, columns, 0)

    def spread_diagonal():
        for n in range(rows // piece):
            first = n * piece
            row = diag_ref[first // tile : first // tile + 1, first % tile : first % tile + piece]
            column = jnp.broadcast_to(row, (tile, piece)).T
            at = slice(n * half_piece, (n + 1) * half_piece)
            diag_full[at, :] = select(column[:half_piece], column[half_piece:])

    def start_interior():
        for n in range(fronts):
            value = jnp.dot(
                inverse_ref[n], load_ref[n], precision=HIGHEST, preferred_element_type=F32
            )
            for s in streams:
                interior[s, n * half_rank : (n + 1) * half_rank, :] = packed(value, s)

    pl.semaphore_wait(barrier, len(peers) + leaves - 1)

    def times(high_ref, low_ref, s, starts, size):
        unit = size // 2
        units = [pl.ds(pl.multiple_of(at + i, unit), unit) for at in starts for i in (0, unit)]
        both = []
        for part in (units[: len(starts)], units[len(starts) :]):
            high = jnp.concatenate([high_ref[at, :] for at in part])
            low = jnp.concatenate([low_ref[at, :] for at in part])
            out = jnp.dot(high, rhs[s], preferred_element_type=F32)
            both.append(out + jnp.dot(low, rhs[s], preferred_element_type=F32))
        return jnp.concatenate(both)

    def times_turned():
        n = depth // 2
        both = []
        for i in (0, n):
            at = slice(i, i + n)
            out = jnp.dot(turned[...], c_high[:, at], preferred_element_type=F32)
            both.append(out + jnp.dot(turned[...], c_low[:, at], preferred_element_type=F32))
        both = [out[:cols] + out[cols:] for out in both]
        return jnp.concatenate([out[:, i : i + tile].T for out in both for i in range(0, n, tile)])

    def arrived(s, n):
        at = pl.ds(pl.multiple_of(n * half_piece, half_piece), half_piece)
        along = direction[s, at, :]
        new = diag_full[at, :] * along + merged[s, n]
        image[s, at, :] = new
        rhs[s, pl.ds(pl.multiple_of(n * piece, piece), piece), :] = operand(new)
        products(s, n, new, (along, residual[s, at, :], new))

    size = half_rank + SUMS

    def projection(s, dz, dy):
        to = front_at(dz, dy)
        return remote(
            w_send.at[s, to, 0:size],
            w_recv.at[s, front, 0:size],
            (w_ssem, w_rsem),
            (s, dz * ny + dy),
            front=to,
        )

    def sums_of(s):
        sums = [piece_sums[s, 0, n] for n in range(SUMS)]
        for i in range(1, rows // piece):
            sums = [total + piece_sums[s, i, n] for n, total in enumerate(sums)]
        sums = [both_sides(total.sum(axis=0, keepdims=True)) for total in sums]
        return jnp.concatenate(sums + [jnp.zeros((EXTRA - SUMS, cols), F32)])

    def project_first():
        out = times_turned()
        for s in streams:
            dots = sums_of(s)
            for j in range(fronts):
                w_send[s, j, 0:half_rank, :] = packed(out[j * rank : (j + 1) * rank], s)
                w_send[s, j, half_rank:, :] = dots
            for dz, dy in peers:
                projection(s, dz, dy).start()

    def project(s):
        dots = sums_of(s)
        span = ny * rank
        for i in range(0, nz, 2):
            steps = z_steps[i : i + 2]
            places = [(z + dz) % nz for dz in steps]
            out = times(t_high, t_low, s, [p * span for p in places], span)
            for n, place in enumerate(places):
                for j in range(ny):
                    at = n * span + j * rank
                    w_send[s, place * ny + j, 0:half_rank, :] = fold(out[at : at + rank])
                    w_send[s, place * ny + j, half_rank:, :] = dots
            for dz in steps:
                for dy in y_steps:
                    if dz or dy:
                        projection(s, dz, dy).start()

    def condense(s, k, is_first):
        w_recv[s, front, 0:size, :] = w_send[s, front, 0:size, :]
        if is_first and s == 0:
            turn(0, rows // 2)
            loads[3].wait()
        for dz, dy in peers:
            projection(s, dz, dy).wait_recv()
        total = w_recv[s, 0]
        for n in range(1, fronts):
            total = total + w_recv[s, n]
        w = total[0:half_rank]
        curvature, cross, square = (total[half_rank + n : half_rank + n + 1] for n in range(SUMS))
        if is_first:
            alpha = beta = None
            rr_ref[s] = square
            tr = td = w
        else:
            rr = rr_ref[s]
            alpha = rr / curvature
            rr_next = rr - 2.0 * alpha * cross + alpha * alpha * square
            beta = rr_next / rr
            rr_ref[s] = rr_next
            tr = tr_ref[s] - alpha * w
            td = tr + beta * td_ref[s]
        tr_ref[s] = tr
        td_ref[s] = td
        coeff = jnp.dot(
            inverse_ref[front],
            jnp.concatenate([td, swap(td)]),
            precision=HIGHEST,
            preferred_element_type=F32,
        )
        coeff = packed(coeff, 0)
        here = pl.ds(pl.multiple_of(front * half_rank, half_rank), half_rank)
        c_send[s] = coeff
        c_full[k, s, here, :] = coeff
        spread = [
            send(
                c_send.at[s],
                c_full.at[k, s, here],
                (c_ssem, c_rsem),
                (s, dz * ny + dy),
                front=front_at(dz, dy),
            )
            for dz, dy in peers
        ]
        return alpha, beta, (td * coeff).reshape(-1, 8, cols).sum(axis=0), spread

    def advance(s, alpha, beta):
        for i in range(0, rows // 2, tile):
            at = slice(i, i + tile)
            x_ref[s, at, :] += alpha * direction[s, at, :]
            res = residual[s, at, :] - alpha * image[s, at, :]
            residual[s, at, :] = res
            direction[s, at, :] = res + beta * direction[s, at, :]

    def subtract(s, k, step):
        for i in range(0, depth // 2, tile):
            at = slice(i, i + tile)
            interior[s, at, :] = interior[s, at, :] - step * c_full[k, s, at, :]

    def finish(s, k, alpha, beta, is_first):
        if not is_first:
            advance(s, alpha, beta)
            subtract(s, k - 1, alpha)
        elif s == 0:
            for copy in (loads[2], loads[4]):
                copy.wait()
            turn(rows // 2, rows)
        else:
            spread_diagonal()
            start_interior()
        for dz, dy in peers:
            projection(s, dz, dy).wait_send()

    def merge(s, k, spread):
        for copy in spread:
            copy.wait_recv()
        for n in range(fronts):
            rhs[s, n * rank : (n + 1) * rank, :] = operand(
                c_full[k, s, n * half_rank : (n + 1) * half_rank, :]
            )

        def field(pieces):
            out = times(c_high, c_low, s, [n * piece for n in pieces], piece)
            return [fold(out[i * piece : (i + 1) * piece]) for i in range(len(pieces))]

        sent = []
        ends = (other, core)
        for at_core, value in zip(ends, field([piece_at(far, n) for n in ends])):
            far_send[s, at_core] = value
        for n, at_core in enumerate(ends):
            sent.append(
                send(
                    far_send.at[s, at_core],
                    far_recv.at[s, core],
                    (f_ssem, f_rsem),
                    (s, 1 - n),
                    leaf=leaf_at(far, at_core),
                )
            )
        steps = near + [0]
        for d, value in zip(steps, field([piece_at(d, other) for d in steps])):
            half_send[s, d] = value
        swapped = [
            send(half_send.at[s, d], half_recv.at[s, d], (h_ssem, h_rsem), (s, d), leaf=partner)
            for d in steps
        ]
        for d, value in zip(steps, field([piece_at(d, core) for d in steps])):
            own_part[s, d] = value
        for copy in spread:
            copy.wait_send()
        for d, copy in zip(steps, swapped):
            copy.wait_recv()
            if d:
                near_send[s, d] = own_part[s, d] + half_recv[s, d]
                sent.append(
                    send(
                        near_send.at[s, d],
                        near_recv.at[s, d],
                        (n_ssem, n_rsem),
                        (s, d),
                        leaf=leaf_at(d, core),
                    )
                )
        return sent, swapped

    def gather(s, sent, swapped):
        total = own_part[s, 0] + half_recv[s, 0]
        for copy in sent:
            copy.wait_recv()
        for d in near:
            total = total + near_recv[s, d]
        for n in range(CORES):
            total = total + far_recv[s, n]
        mine = piece_at(0, core)
        merged[s, mine] = total
        here = merged.at[s, mine]
        gathered = {
            d: send(here, here, (m_ssem, m_rsem), (s, d), leaf=leaf_at(d, core))
            for d in [far] + near
        }
        passed = {0: send(here, here, (p_ssem, p_rsem), (s, 0), leaf=partner)}
        arrived(s, mine)
        for copy in sent + swapped:
            copy.wait_send()
        return gathered, passed

    def collect(s, gathered, passed):
        passed[0].wait_recv()
        arrived(s, piece_at(0, other))
        for d in near + [far]:
            gathered[d].wait_recv()
            at = merged.at[s, piece_at(nx - d, core)]
            passed[d] = send(at, at, (p_ssem, p_rsem), (s, d), leaf=partner)
            arrived(s, piece_at(nx - d, core))
        for d in near + [far]:
            passed[d].wait_recv()
            arrived(s, piece_at(nx - d, other))
        for copy in list(gathered.values()) + list(passed.values()):
            copy.wait_send()

    def iterate(k, is_first):
        spreads = []
        for s in streams:
            alpha, beta, _, spread = condense(s, k, is_first)
            spreads.append(spread)
            finish(s, k, alpha, beta, is_first)
        moves = [merge(s, k, spreads[s]) for s in streams]
        moves = [gather(s, *moves[s]) for s in streams]
        for s in streams:
            collect(s, *moves[s])
            project(s)
        return 0

    project_first()
    iterate(0, True)
    lax.fori_loop(1, ITERS - 1, lambda k, _: iterate(k, False), 0)

    end = ITERS - 1
    ends = [condense(s, end, False) for s in streams]

    def both_streams(values):
        return select(*(both_sides(value) for value in values))

    own = both_streams([own for _, _, own, _ in ends])
    q_send[...] = own
    q_recv[leaf] = own
    over_leaf = [
        send(
            q_send, q_recv.at[leaf], (q_ssem, q_rsem), d, leaf=(leaf + d) % leaves
        )
        for d in range(1, leaves)
    ]
    totals = []
    for s, (alpha, beta, _, _) in enumerate(ends):
        advance(s, alpha, beta)
        q = jnp.zeros((8, cols), F32)
        for i in range(0, rows // 2, tile):
            new = direction[s, i : i + tile, :]
            q = q + (diag_full[i : i + tile, :] * new * new).reshape(-1, 8, cols).sum(axis=0)
        totals.append(q)
    q = both_streams(totals)
    for copy in over_leaf:
        copy.wait_recv()
    for n in range(leaves):
        q = q + q_recv[n]
    g_send[...] = q
    g_recv[front] = q
    over_front = [
        send(
            g_send,
            g_recv.at[front],
            (g_ssem, g_rsem),
            dz * ny + dy,
            front=front_at(dz, dy),
        )
        for dz, dy in peers
    ]
    for s, (alpha, _, _, _) in enumerate(ends):
        subtract(s, end - 1, alpha)

    def widen(n, _):
        at = pl.ds(pl.multiple_of(n * half_piece, half_piece), half_piece)
        to = pl.ds(pl.multiple_of(n * piece, piece), piece)
        x_out[to, :] = full(x_ref[0, at, :], x_ref[1, at, :])
        direction_out[to, :] = full(direction[0, at, :], direction[1, at, :])
        return 0

    lax.fori_loop(0, rows // piece, widen, 0)

    def widen_interior(n, _):
        at = pl.ds(pl.multiple_of(n * half_rank, half_rank), half_rank)
        to = pl.ds(pl.multiple_of(n * rank, rank), rank)
        interior_out[to, :] = full(interior[0, at, :], interior[1, at, :])
        return 0

    lax.fori_loop(0, fronts, widen_interior, 0)
    for s, (_, _, _, spread) in enumerate(ends):
        for dz, dy in peers:
            projection(s, dz, dy).wait_send()
        for copy in spread:
            copy.wait_recv()
    for n in range(fronts):
        at = slice(n * half_rank, (n + 1) * half_rank)
        last_out[n * rank : (n + 1) * rank, :] = full(c_full[end, 0, at, :], c_full[end, 1, at, :])
    for copy in over_front:
        copy.wait_recv()
    q = g_recv[0]
    for n in range(1, fronts):
        q = q + g_recv[n]
    step_ref[...] = select(rr_ref[0], rr_ref[1]) / q.sum(axis=0, keepdims=True)
    for _, _, _, spread in ends:
        for copy in spread:
            copy.wait_send()
    for copy in over_leaf + over_front:
        copy.wait_send()


def per_device(sources, order, diagonal, coupling, interior_inverse, interior_load, grid=(NZ, NY, NX)):
    nz, ny, nx = grid
    fronts, leaves = nz * ny, nx * CORES
    rows, cols = sources.shape
    depth = coupling.shape[1]
    blocks, rank = interior_inverse.shape[:2]
    assert blocks == fronts and depth == blocks * rank
    piece = rows // 2 // nx
    vmem = pl.BlockSpec(memory_space=pltpu.VMEM)
    dma = pltpu.SemaphoreType.DMA
    field = pltpu.VMEM((rows, cols), F32)
    halves = pltpu.VMEM((STREAMS, rows // 2, cols), F32)
    hbm = pl.BlockSpec(memory_space=pltpu.HBM)
    whole = jax.ShapeDtypeStruct((rows, cols), F32)
    inner = jax.ShapeDtypeStruct((depth, cols), F32)
    x, direction, interior, coeff, step = pl.pallas_call(
        functools.partial(front_solve, grid),
        out_shape=(whole, whole, inner, inner, jax.ShapeDtypeStruct((1, cols), F32)),
        in_specs=[hbm] * 6,
        out_specs=(vmem,) * 5,
        scratch_shapes=[
            pltpu.SMEM((rows,), jnp.int32),
            field,
            pltpu.VMEM((rows // 128, 128), F32),
            pltpu.VMEM(interior_inverse.shape, F32),
            pltpu.VMEM(interior_load.shape, F32),
            pltpu.VMEM((rows, depth), F32),
            pltpu.VMEM((rows, depth), BF16),
            pltpu.VMEM((rows, depth), BF16),
            pltpu.VMEM((depth, rows), BF16),
            pltpu.VMEM((depth, rows), BF16),
            pltpu.VMEM((STREAMS, max(rows, depth), cols), BF16),
            pltpu.VMEM((2 * cols, rows), BF16),
            field,
            halves,
            halves,
            halves,
            halves,
            pltpu.VMEM((STREAMS, depth // 2, cols), F32),
            pltpu.VMEM((rows // 2, cols), F32),
            pltpu.VMEM((STREAMS, fronts, rank // 2 + EXTRA, cols), F32),
            pltpu.VMEM((STREAMS, fronts, rank // 2 + EXTRA, cols), F32),
            pltpu.VMEM((STREAMS, rank // 2, cols), F32),
            pltpu.VMEM((ITERS, STREAMS, depth // 2, cols), F32),
            pltpu.VMEM((STREAMS, nx, piece // 2, cols), F32),
            pltpu.VMEM((STREAMS, nx, piece // 2, cols), F32),
            pltpu.VMEM((STREAMS, CORES, piece // 2, cols), F32),
            pltpu.VMEM((STREAMS, CORES, piece // 2, cols), F32),
            pltpu.VMEM((STREAMS, nx, piece // 2, cols), F32),
            pltpu.VMEM((STREAMS, nx, piece // 2, cols), F32),
            pltpu.VMEM((STREAMS, nx, piece // 2, cols), F32),
            pltpu.VMEM((STREAMS, CORES * nx, piece // 2, cols), F32),
            pltpu.VMEM((STREAMS, CORES * nx, SUMS, 8, cols), F32),
            pltpu.VMEM((STREAMS, rank // 2, cols), F32),
            pltpu.VMEM((STREAMS, rank // 2, cols), F32),
            pltpu.VMEM((STREAMS, 1, cols), F32),
            pltpu.VMEM((8, cols), F32),
            pltpu.VMEM((leaves, 8, cols), F32),
            pltpu.VMEM((8, cols), F32),
            pltpu.VMEM((fronts, 8, cols), F32),
            dma((5,)),
            dma((min(8, rows // 128),)),
            dma((STREAMS, fronts)),
            dma((STREAMS, fronts)),
            dma((STREAMS, fronts)),
            dma((STREAMS, fronts)),
            dma((STREAMS, nx)),
            dma((STREAMS, nx)),
            dma((STREAMS, CORES)),
            dma((STREAMS, CORES)),
            dma((STREAMS, nx)),
            dma((STREAMS, nx)),
            dma((STREAMS, nx)),
            dma((STREAMS, nx)),
            dma((STREAMS, nx)),
            dma((STREAMS, nx)),
            dma((leaves,)),
            dma((leaves,)),
            dma((fronts,)),
            dma((fronts,)),
        ],
        compiler_params=pltpu.CompilerParams(
            collective_id=0, has_side_effects=True, vmem_limit_bytes=48 << 20
        ),
        name="front_solve",
    )(
        *(
            pltpu.with_memory_space_constraint(value, pltpu.HBM)
            for value in (
                order,
                sources,
                diagonal.reshape(rows // 128, 128),
                coupling,
                interior_inverse,
                interior_load,
            )
        )
    )
    interior = interior - step * coeff
    return x + step * direction, interior.reshape(interior_load.shape)


def solution(mesh):
    in_specs = (
        P(("wave", "front"), None),
        P("front"),
        P(("wave", "front")),
        P(("wave", "front"), "leaf"),
        P(("wave", "leaf"), None, None),
        P(("wave", "leaf"), None, None),
    )
    out_specs = (P(("wave", "front"), None), P(("wave", "leaf"), None, None))
    return jax.shard_map(
        per_device, mesh=mesh, in_specs=in_specs, out_specs=out_specs, check_vma=False
    )
```

time: 127 us -> 114 us (0.90)
  Pallas kernels: 125 us -> 112 us
    pallas_call x1, Pallas kernels: 125 us -> 112 us  [per_device(): pl.pallas_call(functools.partial(front_solve, grid), out_shape=(whole, wh...]
where the time goes in v2:
time: 114 us
  Pallas kernels  112 us (98%)
    pallas_call x1, Pallas kernels, per_device(): pl.pallas_call(functools.partial(front_solve, grid), out_shape=(whole, wh...  112 us

profile of v2, /device:TPU:1, one launch (start us, length us, event | category | flops | bytes accessed | tf_op | source)
XLA Modules:
  0.0 113.9 jit_solution(13234978318451259813)
XLA Ops:
  0.6 112.2 %front_solve.1 = (f32[1024,128]{1,0:T(8,128)S(1)}, f32[1024,128]{1,0:T(8,128)S(1)}, f32[1024,128]{1,0:T(8,128)S(1)}, f32[1024,128]{1,0:T(8,128)S(1)}, f32[1,128]{1,0:T(1,128)S(1)}) custom-call(s32[1024]{0:T(1024)} %order_hbm.1, f32[1024,128]{1,0:T(8,128)} %sources_hbm.1, f32[8,128]{1,0:T(8,128)} %bitcast.5, f32[1024,1024]{1,0:T(8,128)} %coupling_hbm.1, ...), custom_call_target="tpu_custom_call" | custom-call | tf_op jit(solution)/shard_map/front_solve/pallas_call | solution.py:624
  112.8 1.1 multiply_subtract_fusion

commit v3 on v2

--- a/solution.py
+++ b/solution.py
@@ -92,6 +92,8 @@
     n_rsem,
     m_ssem,
     m_rsem,
+    o_ssem,
+    o_rsem,
     p_ssem,
     p_rsem,
     q_ssem,
@@ -205,17 +207,29 @@
     for copy in loads[:2]:
         copy.wait()
 
-    def take(i, _):
-        for j in range(16):
-            at = i * 16 + j
-            loads_ref[pl.ds(at, 1), :] = sources_ref[pl.ds(order_ref[at] & (rows - 1), 1), :]
-        return 0
-
-    lax.fori_loop(0, rows // 16, take, 0)
+    for i, copy in enumerate(stages):
+        copy.wait()
+
+        def prepare(j, _, i=i):
+            first = i * step_rows + j * 16
+            at = pl.ds(pl.multiple_of(first, 16), 16)
+            high, low = split(stage[at, :])
+            c_high[at, :] = high
+            c_low[at, :] = low
+            for n in range(16):
+                row = pl.ds(order_ref[first + n] & (rows - 1), 1)
+                loads_ref[pl.ds(first + n, 1), :] = sources_ref[row, :]
+            return 0
+
+        lax.fori_loop(0, step_rows // 16, prepare, 0)
+    square = jnp.zeros((8, cols), F32)
     for i in range(0, rows, tile):
         high, low = split(loads_ref[i : i + tile, :].T)
         turned[0:cols, i : i + tile] = high
         turned[cols:, i : i + tile] = low
+        block = loads_ref[i : i + tile, :]
+        square = square + (block * block).reshape(-1, 8, cols).sum(axis=0)
+    square = square.sum(axis=0, keepdims=True)
 
     def start_fields(n, _):
         block = loads_ref[pl.ds(pl.multiple_of(n * piece, piece), piece), :]
@@ -226,22 +240,7 @@
             residual[s, at, :] = value
             direction[s, at, :] = value
             x_ref[s, at, :] = jnp.zeros_like(value)
-            products(s, n, value, (value,) * SUMS)
         return 0
-
-    lax.fori_loop(0, rows // piece, start_fields, 0)
-
-    for i, copy in enumerate(stages):
-        copy.wait()
-
-        def divide(j, _, i=i):
-            at = pl.ds(pl.multiple_of(i * step_rows + j * 16, 16), 16)
-            high, low = split(stage[at, :])
-            c_high[at, :] = high
-            c_low[at, :] = low
-            return 0
-
-        lax.fori_loop(0, step_rows // 16, divide, 0)
 
     def turn(start, stop):
         def columns(j, _):
@@ -323,14 +322,16 @@
     def project_first():
         out = times_turned()
         for s in streams:
-            dots = sums_of(s)
+            norm = select(square, swap(square)) if s == 0 else select(swap(square), square)
+            dots = jnp.concatenate([norm] * SUMS + [jnp.zeros((EXTRA - SUMS, cols), F32)])
             for j in range(fronts):
                 w_send[s, j, 0:half_rank, :] = packed(out[j * rank : (j + 1) * rank], s)
                 w_send[s, j, half_rank:, :] = dots
             for dz, dy in peers:
                 projection(s, dz, dy).start()
-
-    def project(s):
+        lax.fori_loop(0, rows // piece, start_fields, 0)
+
+    def project(s, between=None):
         dots = sums_of(s)
         span = ny * rank
         for i in range(0, nz, 2):
@@ -346,6 +347,8 @@
                 for dy in y_steps:
                     if dz or dy:
                         projection(s, dz, dy).start()
+            if between and i:
+                between()
 
     def condense(s, k, is_first):
         w_recv[s, front, 0:size, :] = w_send[s, front, 0:size, :]
@@ -434,6 +437,17 @@
             out = times(c_high, c_low, s, [n * piece for n in pieces], piece)
             return [fold(out[i * piece : (i + 1) * piece]) for i in range(len(pieces))]
 
+        def swap_over(d):
+            return send(
+                half_send.at[s, d], half_recv.at[s, d], (h_ssem, h_rsem), (s, d), leaf=partner
+            )
+
+        swapped = {}
+        if near:
+            for d, value in zip(near, field([piece_at(d, other) for d in near])):
+                half_send[s, d] = value
+            for d in near:
+                swapped[d] = swap_over(d)
         sent = []
         ends = (other, core)
         for at_core, value in zip(ends, field([piece_at(far, n) for n in ends])):
@@ -449,32 +463,29 @@
                 )
             )
         steps = near + [0]
-        for d, value in zip(steps, field([piece_at(d, other) for d in steps])):
-            half_send[s, d] = value
-        swapped = [
-            send(half_send.at[s, d], half_recv.at[s, d], (h_ssem, h_rsem), (s, d), leaf=partner)
-            for d in steps
-        ]
-        for d, value in zip(steps, field([piece_at(d, core) for d in steps])):
+        values = field([piece_at(0, other)] + [piece_at(d, core) for d in steps])
+        half_send[s, 0] = values[0]
+        swapped[0] = swap_over(0)
+        for d, value in zip(steps, values[1:]):
             own_part[s, d] = value
+        for d in near:
+            swapped[d].wait_recv()
+            near_send[s, d] = own_part[s, d] + half_recv[s, d]
+            sent.append(
+                send(
+                    near_send.at[s, d],
+                    near_recv.at[s, d],
+                    (n_ssem, n_rsem),
+                    (s, d),
+                    leaf=leaf_at(d, core),
+                )
+            )
         for copy in spread:
             copy.wait_send()
-        for d, copy in zip(steps, swapped):
-            copy.wait_recv()
-            if d:
-                near_send[s, d] = own_part[s, d] + half_recv[s, d]
-                sent.append(
-                    send(
-                        near_send.at[s, d],
-                        near_recv.at[s, d],
-                        (n_ssem, n_rsem),
-                        (s, d),
-                        leaf=leaf_at(d, core),
-                    )
-                )
         return sent, swapped
 
     def gather(s, sent, swapped):
+        swapped[0].wait_recv()
         total = own_part[s, 0] + half_recv[s, 0]
         for copy in sent:
             copy.wait_recv()
@@ -486,27 +497,34 @@
         merged[s, mine] = total
         here = merged.at[s, mine]
         gathered = {
-            d: send(here, here, (m_ssem, m_rsem), (s, d), leaf=leaf_at(d, core))
-            for d in [far] + near
+            d: send(here, here, (m_ssem, m_rsem), (s, d), leaf=leaf_at(d, core)) for d in near
         }
+        straight = [
+            send(here, here, (o_ssem, o_rsem), (s, n), leaf=leaf_at(far, at_core))
+            for n, at_core in enumerate((core, other))
+        ]
         passed = {0: send(here, here, (p_ssem, p_rsem), (s, 0), leaf=partner)}
         arrived(s, mine)
-        for copy in sent + swapped:
+        for copy in sent + list(swapped.values()):
             copy.wait_send()
-        return gathered, passed
-
-    def collect(s, gathered, passed):
-        passed[0].wait_recv()
-        arrived(s, piece_at(0, other))
-        for d in near + [far]:
+        return gathered, straight, passed
+
+    def pass_on(s, gathered, straight, passed):
+        for d in near:
             gathered[d].wait_recv()
             at = merged.at[s, piece_at(nx - d, core)]
             passed[d] = send(at, at, (p_ssem, p_rsem), (s, d), leaf=partner)
+
+    def collect(s, gathered, straight, passed):
+        for d in near:
             arrived(s, piece_at(nx - d, core))
-        for d in near + [far]:
+        for d in [0] + near:
             passed[d].wait_recv()
             arrived(s, piece_at(nx - d, other))
-        for copy in list(gathered.values()) + list(passed.values()):
+        for copy, at_core in zip(straight, (core, other)):
+            copy.wait_recv()
+            arrived(s, piece_at(far, at_core))
+        for copy in list(gathered.values()) + straight + list(passed.values()):
             copy.wait_send()
 
     def iterate(k, is_first):
@@ -517,9 +535,11 @@
             finish(s, k, alpha, beta, is_first)
         moves = [merge(s, k, spreads[s]) for s in streams]
         moves = [gather(s, *moves[s]) for s in streams]
-        for s in streams:
-            collect(s, *moves[s])
-            project(s)
+        pass_on(0, *moves[0])
+        collect(0, *moves[0])
+        project(0, lambda: pass_on(1, *moves[1]))
+        collect(1, *moves[1])
+        project(1)
         return 0
 
     project_first()
@@ -680,6 +700,8 @@
             dma((STREAMS, nx)),
             dma((STREAMS, nx)),
             dma((STREAMS, nx)),
+            dma((STREAMS, CORES)),
+            dma((STREAMS, CORES)),
             dma((STREAMS, nx)),
             dma((STREAMS, nx)),
             dma((leaves,)),

time: 114 us -> 110 us (0.965)
  Pallas kernels: 112 us -> 109 us
    pallas_call x1, Pallas kernels: 112 us -> 109 us  [per_device(): pl.pallas_call(functools.partial(front_solve, grid), out_shape=(whole, wh...]
where the time goes in v3:
time: 110 us; the launch traced here: 111 us
  Pallas kernels  109 us (99%)
    pallas_call x1, Pallas kernels, per_device(): pl.pallas_call(functools.partial(front_solve, grid), out_shape=(whole, wh...  109 us

profile of v3, /device:TPU:1, one launch (start us, length us, event | category | flops | bytes accessed | tf_op | source)
XLA Modules:
  0.0 111.0 jit_solution(14217641533534342680)
XLA Ops:
  0.6 109.3 %front_solve.1 = (f32[1024,128]{1,0:T(8,128)S(1)}, f32[1024,128]{1,0:T(8,128)S(1)}, f32[1024,128]{1,0:T(8,128)S(1)}, f32[1024,128]{1,0:T(8,128)S(1)}, f32[1,128]{1,0:T(1,128)S(1)}) custom-call(s32[1024]{0:T(1024)} %order_hbm.1, f32[1024,128]{1,0:T(8,128)} %sources_hbm.1, f32[8,128]{1,0:T(8,128)} %bitcast.5, f32[1024,1024]{1,0:T(8,128)} %coupling_hbm.1, ...), custom_call_target="tpu_custom_call" | custom-call | tf_op jit(solution)/shard_map/front_solve/pallas_call | solution.py:644
  109.9 1.1 multiply_subtract_fusion

commit v4 on v3

--- a/solution.py
+++ b/solution.py
@@ -120,6 +120,10 @@
     far = nx // 2
     near = [d for d in range(1, nx) if d != far]
     peers = [(dz, dy) for dz in z_steps for dy in y_steps if dz or dy]
+    peers.sort(key=lambda d: -min(d[0], nz - d[0]) - min(d[1], ny - d[1]))
+
+    chips = [(dx, dz, dy) for dx in far_first(nx) for dz in z_steps for dy in y_steps if dx or dz or dy]
+    chips.sort(key=lambda d: -sum(min(i, n - i) for i, n in zip(d, (nx, nz, ny))))
 
     def front_at(dz, dy):
         return ((z + dz) % nz) * ny + (y + dy) % ny
@@ -199,6 +203,11 @@
         pl.semaphore_signal(barrier, inc=1, device_id={"front": front_at(dz, dy)})
     for d in range(1, leaves):
         pl.semaphore_signal(barrier, inc=1, device_id={"leaf": (leaf + d) % leaves})
+    for dx, dz, dy in chips:
+        if dx and (dz or dy):
+            pl.semaphore_signal(
+                barrier, inc=1, device_id={"leaf": leaf_at(dx, core), "front": front_at(dz, dy)}
+            )
 
     def products(s, n, im, others):
         for i, field in enumerate(others):
@@ -269,7 +278,7 @@
             for s in streams:
                 interior[s, n * half_rank : (n + 1) * half_rank, :] = packed(value, s)
 
-    pl.semaphore_wait(barrier, len(peers) + leaves - 1)
+    pl.semaphore_wait(barrier, len(peers) + leaves - 1 + (nx - 1) * len(peers))
 
     def times(high_ref, low_ref, s, starts, size):
         unit = size // 2
@@ -343,10 +352,9 @@
                     at = n * span + j * rank
                     w_send[s, place * ny + j, 0:half_rank, :] = fold(out[at : at + rank])
                     w_send[s, place * ny + j, half_rank:, :] = dots
-            for dz in steps:
-                for dy in y_steps:
-                    if dz or dy:
-                        projection(s, dz, dy).start()
+            for dz, dy in peers:
+                if dz in steps:
+                    projection(s, dz, dy).start()
             if between and i:
                 between()
 
@@ -552,15 +560,11 @@
     def both_streams(values):
         return select(*(both_sides(value) for value in values))
 
-    own = both_streams([own for _, _, own, _ in ends])
-    q_send[...] = own
-    q_recv[leaf] = own
-    over_leaf = [
-        send(
-            q_send, q_recv.at[leaf], (q_ssem, q_rsem), d, leaf=(leaf + d) % leaves
-        )
-        for d in range(1, leaves)
-    ]
+    own = both_streams([own for _, _, own, _ in ends]).sum(axis=0, keepdims=True)
+    q_send[0:1, :] = own
+    over_chip = send(
+        q_send.at[0:1], q_recv.at[0:1], (q_ssem, q_rsem), 0, leaf=partner
+    )
     totals = []
     for s, (alpha, beta, _, _) in enumerate(ends):
         advance(s, alpha, beta)
@@ -569,22 +573,22 @@
             new = direction[s, i : i + tile, :]
             q = q + (diag_full[i : i + tile, :] * new * new).reshape(-1, 8, cols).sum(axis=0)
         totals.append(q)
-    q = both_streams(totals)
-    for copy in over_leaf:
-        copy.wait_recv()
-    for n in range(leaves):
-        q = q + q_recv[n]
-    g_send[...] = q
-    g_recv[front] = q
-    over_front = [
+    q = both_streams(totals).sum(axis=0, keepdims=True) * (1.0 / nx)
+    over_chip.wait_recv()
+    q = q + (own + q_recv[0:1, :])
+    g_send[0:1, :] = q
+    place = x * fronts + front
+    g_recv[place, 0:1, :] = q
+    over_all = [
         send(
-            g_send,
-            g_recv.at[front],
+            g_send.at[0:1],
+            g_recv.at[place, 0:1],
             (g_ssem, g_rsem),
-            dz * ny + dy,
+            (dx * nz + dz) * ny + dy,
+            leaf=leaf_at(dx, core),
             front=front_at(dz, dy),
         )
-        for dz, dy in peers
+        for dx, dz, dy in chips
     ]
     for s, (alpha, _, _, _) in enumerate(ends):
         subtract(s, end - 1, alpha)
@@ -613,16 +617,16 @@
     for n in range(fronts):
         at = slice(n * half_rank, (n + 1) * half_rank)
         last_out[n * rank : (n + 1) * rank, :] = full(c_full[end, 0, at, :], c_full[end, 1, at, :])
-    for copy in over_front:
+    for copy in over_all:
         copy.wait_recv()
-    q = g_recv[0]
-    for n in range(1, fronts):
-        q = q + g_recv[n]
-    step_ref[...] = select(rr_ref[0], rr_ref[1]) / q.sum(axis=0, keepdims=True)
+    q = g_recv[0, 0:1, :]
+    for n in range(1, nx * fronts):
+        q = q + g_recv[n, 0:1, :]
+    step_ref[...] = select(rr_ref[0], rr_ref[1]) / q
     for _, _, _, spread in ends:
         for copy in spread:
             copy.wait_send()
-    for copy in over_leaf + over_front:
+    for copy in [over_chip] + over_all:
         copy.wait_send()
 
 
@@ -683,9 +687,9 @@
             pltpu.VMEM((STREAMS, rank // 2, cols), F32),
             pltpu.VMEM((STREAMS, 1, cols), F32),
             pltpu.VMEM((8, cols), F32),
-            pltpu.VMEM((leaves, 8, cols), F32),
             pltpu.VMEM((8, cols), F32),
-            pltpu.VMEM((fronts, 8, cols), F32),
+            pltpu.VMEM((8, cols), F32),
+            pltpu.VMEM((nx * fronts, 8, cols), F32),
             dma((5,)),
             dma((min(8, rows // 128),)),
             dma((STREAMS, fronts)),
@@ -704,10 +708,10 @@
             dma((STREAMS, CORES)),
             dma((STREAMS, nx)),
             dma((STREAMS, nx)),
-            dma((leaves,)),
-            dma((leaves,)),
-            dma((fronts,)),
-            dma((fronts,)),
+            dma((1,)),
+            dma((1,)),
+            dma((nx * fronts,)),
+            dma((nx * fronts,)),
         ],
         compiler_params=pltpu.CompilerParams(
             collective_id=0, has_side_effects=True, vmem_limit_bytes=48 << 20

time: 110 us -> 111 us (level); the launches traced: 111 us -> 111 us
  no operation moved by 1% of the time
where the time goes in v4:
time: 111 us
  Pallas kernels  109 us (98%)
    pallas_call x1, Pallas kernels, per_device(): pl.pallas_call(functools.partial(front_solve, grid), out_shape=(whole, wh...  109 us

profile of v4, /device:TPU:1, one launch (start us, length us, event | category | flops | bytes accessed | tf_op | source)
XLA Modules:
  0.0 110.7 jit_solution(1619170038583642721)
XLA Ops:
  0.6 109.0 %front_solve.1 = (f32[1024,128]{1,0:T(8,128)S(1)}, f32[1024,128]{1,0:T(8,128)S(1)}, f32[1024,128]{1,0:T(8,128)S(1)}, f32[1024,128]{1,0:T(8,128)S(1)}, f32[1,128]{1,0:T(1,128)S(1)}) custom-call(s32[1024]{0:T(1024)} %order_hbm.1, f32[1024,128]{1,0:T(8,128)} %sources_hbm.1, f32[8,128]{1,0:T(8,128)} %bitcast.5, f32[1024,1024]{1,0:T(8,128)} %coupling_hbm.1, ...), custom_call_target="tpu_custom_call" | custom-call | tf_op jit(solution)/shard_map/front_solve/pallas_call | solution.py:648
  109.6 1.1 multiply_subtract_fusion

commit v5 on v4

--- a/solution.py
+++ b/solution.py
@@ -384,13 +384,10 @@
             td = tr + beta * td_ref[s]
         tr_ref[s] = tr
         td_ref[s] = td
-        coeff = jnp.dot(
-            inverse_ref[front],
-            jnp.concatenate([td, swap(td)]),
-            precision=HIGHEST,
-            preferred_element_type=F32,
-        )
-        coeff = packed(coeff, 0)
+        high, low = split(inverse_ref[front])
+        right = operand(td)
+        coeff = jnp.dot(high, right, preferred_element_type=F32)
+        coeff = fold(coeff + jnp.dot(low, right, preferred_element_type=F32))
         here = pl.ds(pl.multiple_of(front * half_rank, half_rank), half_rank)
         c_send[s] = coeff
         c_full[k, s, here, :] = coeff

time: 111 us -> 108 us (0.973)
  Pallas kernels: 109 us -> 107 us
    pallas_call x1, Pallas kernels: 109 us -> 107 us  [per_device(): pl.pallas_call(functools.partial(front_solve, grid), out_shape=(whole, wh...]
where the time goes in v5:
time: 108 us
  Pallas kernels  107 us (99%)
    pallas_call x1, Pallas kernels, per_device(): pl.pallas_call(functools.partial(front_solve, grid), out_shape=(whole, wh...  107 us

profile of v5, /device:TPU:1, one launch (start us, length us, event | category | flops | bytes accessed | tf_op | source)
XLA Modules:
  0.0 108.3 jit_solution(288453660306982781)
XLA Ops:
  0.6 106.6 %front_solve.1 = (f32[1024,128]{1,0:T(8,128)S(1)}, f32[1024,128]{1,0:T(8,128)S(1)}, f32[1024,128]{1,0:T(8,128)S(1)}, f32[1024,128]{1,0:T(8,128)S(1)}, f32[1,128]{1,0:T(1,128)S(1)}) custom-call(s32[1024]{0:T(1024)} %order_hbm.1, f32[1024,128]{1,0:T(8,128)} %sources_hbm.1, f32[8,128]{1,0:T(8,128)} %bitcast.5, f32[1024,1024]{1,0:T(8,128)} %coupling_hbm.1, ...), custom_call_target="tpu_custom_call" | custom-call | tf_op jit(solution)/shard_map/front_solve/pallas_call | solution.py:645
  107.2 1.1 multiply_subtract_fusion
